TPU v7x, 128 devices: a whole 4x4x4 slice. The times are simulated.
128 devices in a mesh: row: 8 (over z, core), col: 16 (over y, x).
Axes of the slice: x: 4, y: 4, z: 4, core: 2. Of those that a mesh axis runs over, the one named last changes fastest.
Arguments:
- ainv_anc: bfloat16 [24576, 24576], P('row', 'col'), may hold values from -6 to 6
- l_panel: bfloat16 [1536, 24576], P('col', 'row'), may hold values from -0.078125 to 0.078125
- diag_inv: float32 [1536, 768], P('col', 'row'), may hold values from -6 to 6
- struct_mask: int32 [2, 192], replicated, may hold values 0 or 1
- pieces: float32 [24576, 32, 128], P(('row', 'col')), may hold values from -6 to 6
- tile_owner: int32 [24576, 1], P(('row', 'col')), may hold values from 0 to 127; in each aligned block of 192 rows (0 to 191, 192 to 383, ...) at most 3 rows name the same one
Outputs:
- ainv_upper: bfloat16 [1536, 24576], P('col', 'row')
- ainv_diag: float32 [1536, 768], P('col', 'row')
- moved: float32 [49152, 32, 128], P(('row', 'col'))
Inputs may be any that keep to these rules, and one draw needn't show every extreme that they name: `tile_owner`: among the 192 pieces of one device no owner is named more than 3 times, a bound that some block reaches.
All inputs are finite; a program needn't handle non-finite values.
Results may differ from a plain program's by a relative error of at most 0.015.
Values may be sent and summed in bfloat16 or wider, within the bound.
A program may use at most 128 MiB of HBM per device.

v0:
```python
import jax
import jax.numpy as jnp
from jax import lax
from jax.sharding import PartitionSpec as P

W = 768
AB = 128
SLOT = 3


def broadcast(value, axis, root):
    mine = lax.axis_index(axis) == root
    return lax.psum(jnp.where(mine, value, jnp.zeros_like(value)), axis)


def cut_along(value, dim, count):
    before, after = (value.shape[:dim], value.shape[dim + 1 :])
    return jnp.moveaxis(value.reshape(*before, count, -1, *after), dim, 0)


def sum_at_owner(value, axis, dim):
    parts = cut_along(value, dim, lax.axis_size(axis))
    arrived = lax.all_to_all(parts, axis, split_axis=0, concat_axis=0, tiled=True)
    return arrived.astype(jnp.float32).sum(axis=0)


def joined_along(parts, dim):
    shape = list(parts.shape[1:])
    shape[dim] *= parts.shape[0]
    return jnp.moveaxis(parts, 0, dim).reshape(shape)


def joined_exchange(value, axis, axes, splits, concats):
    sizes = [lax.axis_size(a) for a in axes]
    parts = cut_along(value, splits[0], sizes[0])
    parts = jnp.moveaxis(cut_along(parts, splits[1] + 1, sizes[1]), 0, 1)
    inside = parts.shape[2:]
    parts = parts.reshape(-1, *inside)
    parts = lax.all_to_all(parts, axis, split_axis=0, concat_axis=0, tiled=True)
    parts = joined_along(parts.reshape(*sizes, *inside), concats[0] + 1)
    return joined_along(parts, concats[1])


def local(ainv_anc, l_panel, diag_inv, struct_mask, pieces, tile_owner):
    row_devices = lax.axis_size("row")
    col_devices = lax.axis_size("col")
    row_index = lax.axis_index("row")
    col_index = lax.axis_index("col")
    slab_rows = l_panel.shape[0]
    local_rows = l_panel.shape[1]
    cross_width = ainv_anc.shape[1]
    group_ratio = col_devices // row_devices
    supernode = col_index * slab_rows // W
    block_count = local_rows // AB
    keep_blocks = lax.dynamic_slice(
        struct_mask, (supernode, row_index * block_count), (1, block_count)
    )
    keep_rows = (
        jnp.broadcast_to(keep_blocks[:, :, None], (1, block_count, AB)).reshape(1, local_rows) > 0
    )
    masked = jnp.where(keep_rows, l_panel, jnp.zeros_like(l_panel))
    gathered = lax.all_gather(masked, "col", axis=0, tiled=True)
    offset = col_index % group_ratio * cross_width
    own_cross = lax.dynamic_slice_in_dim(gathered, offset, cross_width, 1)
    cross_rows = broadcast(own_cross, "row", col_index // group_ratio)
    product = lax.psum_scatter(
        lax.dot_general(
            cross_rows, ainv_anc, (((1,), (1,)), ((), ())), preferred_element_type=jnp.float32
        ).astype(jnp.bfloat16),
        "col",
        scatter_dimension=0,
        tiled=True,
    ).astype(jnp.float32)
    upper_rows = jnp.where(keep_rows, -product, jnp.zeros_like(product)).astype(jnp.bfloat16)
    own_block = lax.dynamic_slice_in_dim(gathered, supernode * W, W, 0)
    diag_part = lax.dot_general(
        upper_rows, own_block, (((1,), (1,)), ((), ())), preferred_element_type=jnp.float32
    )
    summed = sum_at_owner(diag_part.astype(jnp.bfloat16), "row", 1)
    ainv_diag = diag_inv - summed
    devices_all = row_devices * col_devices
    owners = tile_owner[:, 0]
    onehot = (owners[:, None] == jnp.arange(devices_all, dtype=jnp.int32)[None, :]).astype(
        jnp.int32
    )
    earlier = jnp.cumsum(onehot, axis=0) - onehot
    rank_in_dest = jnp.sum(earlier * onehot, axis=1)
    slot_index = owners * SLOT + rank_in_dest
    piece_rows = pieces.shape[1]
    piece_cols = pieces.shape[2]
    buffer = (
        jnp.zeros((devices_all * SLOT, piece_rows, piece_cols), jnp.float32)
        .at[slot_index]
        .set(pieces)
    )
    shaped = buffer.reshape(row_devices, col_devices, SLOT, piece_rows, piece_cols)
    arrived = joined_exchange(
        shaped.astype(jnp.bfloat16), ("row", "col"), ("row", "col"), (0, 1), (0, 1)
    ).astype(shaped.dtype)
    moved_pieces = arrived.reshape(devices_all * SLOT, piece_rows, piece_cols)
    return (upper_rows, ainv_diag, moved_pieces)


def solution(mesh):
    in_specs = (
        P("row", "col"),
        P("col", "row"),
        P("col", "row"),
        P(),
        P(("row", "col"), None, None),
        P(("row", "col"), None),
    )
    out_specs = (P("col", "row"), P("col", "row"), P(("row", "col"), None, None))
    return jax.shard_map(local, mesh=mesh, in_specs=in_specs, out_specs=out_specs, check_vma=False)
```

profile of v0, /device:TPU:13, one launch (start us, length us, event | category | flops | bytes accessed | tf_op | source)
XLA Modules:
  0.0 329.3 jit_solution(8603867656916050667)
XLA Ops:
  7.2 0.0 all-gather.2.cloned.1.call-start
  7.2 0.8 compare_bitcast_fusion
  8.0 0.1 broadcast_bitcast_fusion
  8.1 1.9 broadcast_select_fusion
  10.0 0.0 all-gather.2.cloned.1.call-update
  10.0 0.0 all-reduce.3.cloned.1.call-start
  10.1 76.8 %all-gather.2.cloned.1.call-done = bf16[1536,3072]{1,0:T(8,128)(2,1)} async-done(((bf16[96,3072]{1,0:T(8,128)(2,1)}), bf16[1536,3072]{1,0:T(8,128)(2,1)}) %all-gather.2.cloned.1.call-update) | async-done | bytes 9437200 | tf_op jit(solution)/shard_map/all_gather | solution.py:62
  87.0 5.3 %dynamic-slice_select_fusion = bf16[1536,1536]{1,0:T(8,128)(2,1)} fusion(bf16[1536,3072]{1,0:T(8,128)(2,1)} %all-gather.2.cloned.1.call-done, s32[]{:T(128)S(6)} %select_n.53, pred[]{:T(512)S(6)} %eq.27), kind=kLoop, calls=%fused_computation.4 | loop fusion | flops 2359296 | bytes 9437189 | tf_op jit(solution)/shard_map/jit(_where)/select_n | solution.py:13
  92.3 0.0 all-reduce.3.cloned.1.call-update
  92.3 0.0 reduce-scatter.2.cloned.1.call-start
  92.4 74.1 %all-reduce.3.cloned.1.call-done = bf16[1536,1536]{1,0:T(8,128)(2,1)} async-done(((bf16[1536,1536]{1,0:T(8,128)(2,1)}), bf16[1536,1536]{1,0:T(8,128)(2,1)}) %all-reduce.3.cloned.1.call-update) | async-done | bytes 4718608 | tf_op jit(solution)/shard_map/psum | solution.py:13
  166.5 20.3 %convolution_convert_fusion = bf16[1536,3072]{1,0:T(8,128)(2,1)} fusion(bf16[1536,1536]{1,0:T(8,128)(2,1)} %all-reduce.3.cloned.1.call-done, bf16[3072,1536]{1,0:T(8,128)(2,1)} %param.6), kind=kOutput, calls=%fused_computation.1 | convolution fusion | flops 14500233216 | bytes 23592960 | tf_op jit(solution)/shard_map/dot_general | solution.py:67
  186.8 0.0 reduce-scatter.2.cloned.1.call-update
  186.9 0.6 copy-done.3
  187.5 0.1 iota_compare_fusion
  187.6 0.1 fusion.5
  187.9 0.2 fusion.8
  188.1 3.5 %broadcast_in_dim.39 = f32[384,32,128]{2,1,0:T(8,128)} broadcast(f32[]{:T(128)} %constant.65.clone.1), dimensions={} | broadcast | bytes 6291460 | tf_op jit(solution)/shard_map/broadcast_in_dim | solution.py:92
  191.6 23.6 %scatter_fusion = f32[384,32,128]{2,1,0:T(8,128)} fusion(f32[384,32,128]{2,1,0:T(8,128)} %broadcast_in_dim.39, s32[192]{0:T(256)S(1)} %bitcast.46, f32[192,32,128]{2,1,0:T(8,128)S(1)} %copy-done), kind=kCustom, calls=%fused_computation | custom fusion | bytes 9437952 | tf_op jit(solution)/shard_map/scatter | solution.py:94
  215.1 5.4 %convert_element_type.54 = bf16[384,32,128]{2,1,0:T(8,128)(2,1)} convert(f32[384,32,128]{2,1,0:T(8,128)} %scatter_fusion) | non-fusion elementwise | flops 1572864 | bytes 9437184 | tf_op jit(solution)/shard_map/convert_element_type | solution.py:98
  220.5 9.9 %all-to-all-start.1 = ((bf16[128,1,1,3,32,128]{5,4,3,2,1,0:T(8,128)(2,1)}), bf16[128,1,1,3,32,128]{5,4,3,2,1,0:T(8,128)(2,1)S(1)}, u32[]{:S(2)}, u32[]{:S(2)}) async-start(bf16[128,1,1,3,32,128]{5,4,3,2,1,0:T(8,128)(2,1)} %bitcast.38), calls=%async_computation.2 | async-start | bytes 6291456 | tf_op jit(solution)/shard_map/all_to_all | solution.py:39
  230.4 72.3 %reduce-scatter.2.cloned.1.call-done = bf16[96,3072]{1,0:T(8,128)(2,1)} async-done(((bf16[1536,3072]{1,0:T(8,128)(2,1)}), bf16[96,3072]{1,0:T(8,128)(2,1)}) %reduce-scatter.2.cloned.1.call-update) | async-done | bytes 589840 | tf_op jit(solution)/shard_map/reduce_scatter | solution.py:66
  302.6 1.2 select_convert_fusion
  303.9 0.0 copy-start.1
  303.9 0.8 copy-done.1
  304.7 3.9 %fusion.2 = bf16[96,768]{1,0:T(8,128)(2,1)S(1)} fusion(bf16[96,3072]{1,0:T(8,128)(2,1)S(1)} %select_convert_fusion, bf16[1536,3072]{1,0:T(8,128)(2,1)} %all-gather.2.cloned.1.call-done, s32[]{:T(128)S(6)} %select_n.56), kind=kOutput, calls=%fused_computation.7 | convolution fusion | flops 453058560 | bytes 5455876 | tf_op jit(solution)/shard_map/dot_general | solution.py:76
  308.6 0.2 reshape.62
  308.9 0.7 copy.18
  309.6 6.7 %all-to-all-start = ((bf16[8,96,96]{2,1,0:T(8,128)(2,1)}), bf16[8,96,96]{2,1,0:T(8,128)(2,1)S(1)}, u32[]{:S(2)}, u32[]{:S(2)}) async-start(bf16[8,96,96]{2,1,0:T(8,128)(2,1)} %bitcast.34), calls=%async_computation.1 | async-start | bytes 393216 | tf_op jit(solution)/shard_map/all_to_all | solution.py:23
  316.3 3.8 %bitcast_convert_fusion = f32[384,32,128]{2,1,0:T(8,128)} fusion(bf16[128,1,1,3,32,128]{5,4,3,2,1,0:T(8,128)(2,1)S(1)} %all-to-all-done.1), kind=kLoop, calls=%fused_computation.5 | loop fusion | flops 1572864 | bytes 9437184 | tf_op jit(solution)/shard_map/convert_element_type | solution.py:99
  320.1 2.1 all-to-all-done
  322.2 0.6 sub.15
  (15 shorter events, 0.2 us)
Async XLA Ops:
  7.2 79.8 %all-gather.2.cloned.1.call-start = ((), (), s32[]{:S(2)}) async-start(), calls=%async_computation.3 | async-start | bytes 10027008 | tf_op jit(solution)/shard_map/all_gather | solution.py:62
  10.0 156.5 %all-reduce.3.cloned.1.call-start = ((), (), s32[]{:S(2)}) async-start(), calls=%async_computation.4 | async-start | bytes 9437184 | tf_op jit(solution)/shard_map/psum | solution.py:13
  92.3 210.3 %reduce-scatter.2.cloned.1.call-start = ((), (), s32[]{:S(2)}) async-start(), calls=%async_computation.5 | async-start | bytes 10027008 | tf_op jit(solution)/shard_map/reduce_scatter | solution.py:66
  186.8 0.7 copy-start.3
  186.8 4.7 %copy-start = (f32[192,32,128]{2,1,0:T(8,128)S(1)}, f32[192,32,128]{2,1,0:T(8,128)}, u32[]{:S(2)}) copy-start(f32[192,32,128]{2,1,0:T(8,128)} %param.10) | copy-start | bytes 9437188
  220.5 89.1 %all-to-all-start.1 = ((bf16[128,1,1,3,32,128]{5,4,3,2,1,0:T(8,128)(2,1)}), bf16[128,1,1,3,32,128]{5,4,3,2,1,0:T(8,128)(2,1)S(1)}, u32[]{:S(2)}, u32[]{:S(2)}) async-start(bf16[128,1,1,3,32,128]{5,4,3,2,1,0:T(8,128)(2,1)} %bitcast.38), calls=%async_computation.2 | async-start | bytes 6291456 | tf_op jit(solution)/shard_map/all_to_all | solution.py:39
  303.9 0.8 copy-start.1
  309.6 12.6 %all-to-all-start = ((bf16[8,96,96]{2,1,0:T(8,128)(2,1)}), bf16[8,96,96]{2,1,0:T(8,128)(2,1)S(1)}, u32[]{:S(2)}, u32[]{:S(2)}) async-start(bf16[8,96,96]{2,1,0:T(8,128)(2,1)} %bitcast.34), calls=%async_computation.1 | async-start | bytes 393216 | tf_op jit(solution)/shard_map/all_to_all | solution.py:23
  316.3 5.9 %copy-start.2 = (f32[96,96]{1,0:T(8,128)S(1)}, f32[96,96]{1,0:T(8,128)}, u32[]{:S(2)}) copy-start(f32[96,96]{1,0:T(8,128)} %param.8) | copy-start | bytes 110596
Sparse Core Ops, SparseCore 0:
  10.7 76.2 all-gather.1
  92.4 74.0 all-reduce.2
  187.0 115.6 reduce-scatter.1
where the time goes:
time: 334 us; the launch traced here: 329 us
  waiting for transfers between devices  225 us (67%)
  local copies, waits for them, and re-layouts  29.6 us (9%)
  matrix products  24.2 us (7%)
  other arithmetic  19.6 us (6%)
  starting transfers between devices  16.7 us (5%)
  between operations  13.9 us (4%)
    all_gather x1, waiting for transfers between devices, local(): gathered = lax.all_gather(masked, 'col', axis=0, tiled=True)  76.8 us
    psum x1, waiting for transfers between devices, broadcast(): return lax.psum(jnp.where(mine, value, jnp.zeros_like(value)), axis)  74.1 us
    reduce_scatter x1, waiting for transfers between devices, local(): lax.psum_scatter(lax.dot_general(cross_rows, ainv_anc, (((1,), (1,)), (()...  72.3 us
    scatter x1, local copies, waits for them, and re-layouts, local(): buffer = jnp.zeros((devices_all * SLOT, piece_rows, piece_cols), jnp.floa...  23.6 us
    dot_general x1, matrix products, local(): lax.dot_general(cross_rows, ainv_anc, (((1,), (1,)), ((), ())), preferred...  20.3 us
    all_to_all x1, starting transfers between devices, joined_exchange(): parts = lax.all_to_all(parts, axis, split_axis=0, concat_axis=0, tiled=True)  9.86 us
    all_to_all x1, starting transfers between devices, sum_at_owner(): lax.all_to_all(parts, axis, split_axis=0, concat_axis=0, tiled=True)  6.7 us
  transfers between devices with their start and end apart: 5, of which 4 were waited for; matrix products, arithmetic and copies ran while one was open for 13% of the time, Pallas kernels for 0%

commit v1 on v0

v1 whole, which is shorter than its diff:
```python
import jax
import jax.numpy as jnp
from jax import lax
from jax.experimental import pallas as pl
from jax.experimental.pallas import tpu as pltpu
from jax.sharding import PartitionSpec as P

W = 768
AB = 128
SLOT = 3
SIDE = 4
PB = 96
HALF = 1536
QUART = 768
TILE = 256
BF16, F32 = jnp.bfloat16, jnp.float32


def pack_kernel(owner_ref, pieces_ref, out_ref, count_ref):
    devices = out_ref.shape[0] // SLOT

    def clear(i, _):
        out_ref[pl.ds(i * 8, 8)] = jnp.zeros((8, *out_ref.shape[1:]), out_ref.dtype)
        return 0

    lax.fori_loop(0, out_ref.shape[0] // 8, clear, 0)

    def reset(i, _):
        count_ref[i] = 0
        return 0

    lax.fori_loop(0, devices, reset, 0)

    def place(p, _):
        owner = owner_ref[p]
        rank = count_ref[owner]
        count_ref[owner] = rank + 1
        out_ref[owner * SLOT + rank] = pieces_ref[p].astype(out_ref.dtype)
        return 0

    lax.fori_loop(0, pieces_ref.shape[0], place, 0)


def packed(owners, pieces, devices):
    shape = (devices * SLOT, *pieces.shape[1:])
    return pl.pallas_call(
        pack_kernel,
        out_shape=jax.ShapeDtypeStruct(shape, BF16),
        in_specs=[
            pl.BlockSpec(memory_space=pltpu.SMEM),
            pl.BlockSpec(memory_space=pltpu.VMEM),
        ],
        out_specs=pl.BlockSpec(memory_space=pltpu.VMEM),
        scratch_shapes=[pltpu.SMEM((devices,), jnp.int32)],
        name="pack",
    )(owners, pieces)


def invert_kernel(
    mask_ref, a_hbm, panel_ref, dinv_ref, upper_ref, diag_ref,
    zbuf, lm, a, part, in1, tot, in2, usend, ubuf, sendd, recvd,
    a_sem, z_ssem, z_rsem, l_ssem, l_rsem, f_ssem, f_rsem,
    p1_ssem, p1_rsem, p2_ssem, p2_rsem, u_ssem, u_rsem, d_ssem, d_rsem,
):
    r, c = lax.axis_index("row"), lax.axis_index("col")
    z, k = r // 2, r % 2
    y, x = c // SIDE, c % SIDE
    node = c // (W // PB)
    started = []

    def at(row, col):
        return {"row": row, "col": col}

    def send(src, dst, ssem, rsem, row, col):
        return pltpu.make_async_remote_copy(
            src_ref=src, dst_ref=dst, send_sem=ssem, recv_sem=rsem,
            device_id=at(row, col), device_id_type=pl.DeviceIdType.MESH,
        )

    def go(*args):
        copy = send(*args)
        copy.start()
        started.append(copy)

    def arrived(dst, sem):
        send(dst, dst, sem, sem, r, c).wait_recv()

    a_copy = pltpu.make_async_copy(a_hbm, a, a_sem)
    a_copy.start()

    blocks = panel_ref.shape[1] // AB
    for b in range(blocks):
        keep = jnp.full((PB, AB), mask_ref[node, r * blocks + b], jnp.int32) > 0
        value = panel_ref[:, b * AB : (b + 1) * AB].astype(F32)
        h, o = divmod(b * AB, HALF)
        zbuf[z, h, :, o : o + AB] = jnp.where(keep, value, 0.0).astype(BF16)

    zp, zm, zo = (z + 1) % SIDE, (z + 3) % SIDE, (z + 2) % SIDE
    up, down = 2 * zp + k, 2 * zm + k
    go(zbuf.at[z, 0], zbuf.at[z, 0], z_ssem.at[0], z_rsem.at[0], up, c)
    go(zbuf.at[z, 1], zbuf.at[z, 1], z_ssem.at[1], z_rsem.at[1], down, c)
    go(zbuf.at[z, 1], zbuf.at[z, 1], z_ssem.at[2], z_rsem.at[2], up, c)
    go(zbuf.at[z, 0], zbuf.at[z, 0], z_ssem.at[3], z_rsem.at[3], down, c)

    core = (x + y) % 2

    def own_block(zs, h):
        return (SIDE * zs + 2 * k + h == c) & (k == core)

    spread = []

    def to_column(n, zs, h):
        copy = send(
            zbuf.at[zs, h], lm.at[c], l_ssem.at[n], l_rsem.at[c],
            2 * z + core, SIDE * zs + 2 * k + h,
        )
        mine = own_block(zs, h)

        @pl.when(mine)
        def _():
            lm[c] = zbuf[zs, h]

        @pl.when(jnp.logical_not(mine))
        def _():
            copy.start()

        spread.append((copy, mine))

    to_column(0, z, 0)
    to_column(1, z, 1)
    arrived(zbuf.at[zm, 0], z_rsem.at[0])
    go(zbuf.at[zm, 0], zbuf.at[zm, 0], z_ssem.at[4], z_rsem.at[4], up, c)
    arrived(zbuf.at[zp, 1], z_rsem.at[1])
    go(zbuf.at[zp, 1], zbuf.at[zp, 1], z_ssem.at[5], z_rsem.at[5], down, c)
    to_column(2, zm, 0)
    to_column(3, zp, 1)
    arrived(zbuf.at[zm, 1], z_rsem.at[2])
    to_column(4, zm, 1)
    arrived(zbuf.at[zp, 0], z_rsem.at[3])
    to_column(5, zp, 0)
    arrived(zbuf.at[zo, 0], z_rsem.at[4])
    to_column(6, zo, 0)
    arrived(zbuf.at[zo, 1], z_rsem.at[5])
    to_column(7, zo, 1)

    other = 2 * z + 1 - k

    def nth(n, parity):
        yy, xx = n // 2, n % 2
        return SIDE * yy + 2 * xx + (yy + parity) % 2

    def hand_on(n, _):
        b = nth(n, k)

        @pl.when(jnp.logical_not((b == c) & (x // 2 == k)))
        def _():
            arrived(lm.at[b], l_rsem.at[b])

        send(lm.at[b], lm.at[b], f_ssem.at[n], f_rsem.at[b], other, c).start()
        return 0

    lax.fori_loop(0, 8, hand_on, 0)

    def take(n, _):
        b = nth(n, 1 - k)
        arrived(lm.at[b], f_rsem.at[b])
        return 0

    lax.fori_loop(0, 8, take, 0)
    a_copy.wait()

    place = (x, y)

    def neighbour(axis, step):
        if axis == 0:
            return r, SIDE * y + (x + step) % SIDE
        return r, SIDE * ((y + step) % SIDE) + x

    FAR, NEXT, LAST, OWN = range(4)

    def multiply(half, slot, dest):
        across, along = (SIDE, 1) if half == 0 else (1, SIDE)

        def tile(t, _):
            rows = jnp.concatenate([lm[j * across + dest * along] for j in range(SIDE)], axis=0)
            cols = a[pl.ds(pl.multiple_of(half * HALF + t * TILE, TILE), TILE), :]
            value = lax.dot_general(rows, cols, (((1,), (1,)), ((), ())), preferred_element_type=F32)
            per = QUART // TILE
            part[half, slot, t // per, :, pl.ds(pl.multiple_of((t % per) * TILE, TILE), TILE)] = value.astype(BF16)
            return 0

        lax.fori_loop(0, HALF // TILE, tile, 0)

    def hop1(half, slot, piece, n, step):
        go(
            part.at[half, slot, piece], in1.at[half, n], p1_ssem.at[half, n], p1_rsem.at[half, n],
            *neighbour(half, step),
        )

    def add1(half, slot, piece, n):
        arrived(in1.at[half, n], p1_rsem.at[half, n])

        def rows(i, _):
            s = pl.ds(pl.multiple_of(i * 32, 32), 32)
            value = part[half, slot, piece, s, :].astype(F32) + in1[half, n, s, :].astype(F32)
            part[half, slot, piece, s, :] = value.astype(BF16)
            return 0

        lax.fori_loop(0, SIDE * PB // 32, rows, 0)

    for half in range(2):
        multiply(half, FAR, (place[half] + 2) % SIDE)
        hop1(half, FAR, 0, 0, 1)
        hop1(half, FAR, 1, 1, 3)
    for half in range(2):
        multiply(half, NEXT, (place[half] + 1) % SIDE)
        hop1(half, NEXT, 1, 3, 1)
        multiply(half, LAST, (place[half] + 3) % SIDE)
        hop1(half, LAST, 0, 5, 3)
    for half in range(2):
        add1(half, NEXT, 0, 0)
        hop1(half, NEXT, 0, 2, 1)
        add1(half, LAST, 1, 1)
        hop1(half, LAST, 1, 4, 3)
    for half in range(2):
        multiply(half, OWN, place[half])

    def hop2(half, group, piece, n, step):
        go(
            tot.at[half, group, piece], in2.at[half, n], p2_ssem.at[half, n], p2_rsem.at[half, n],
            *neighbour(1 - half, step),
        )

    def add2(half, group, piece, n):
        arrived(in2.at[half, n], p2_rsem.at[half, n])
        value = tot[half, group, piece].astype(F32) + in2[half, n].astype(F32)
        tot[half, group, piece] = value.astype(BF16)

    for half in range(2):
        q = place[1 - half]
        for n in (3, 5, 2, 4):
            arrived(in1.at[half, n], p1_rsem.at[half, n])

        def sums(i, _, half=half):
            s = pl.ds(pl.multiple_of(i * PB, PB), PB)
            for piece, (m, n) in enumerate(((2, 5), (3, 4))):
                value = part[half, OWN, piece, s, :].astype(F32) + in1[half, m, s, :].astype(F32)
                tot[half, i, piece] = (value + in1[half, n, s, :].astype(F32)).astype(BF16)
            return 0

        lax.fori_loop(0, SIDE, sums, 0)
        hop2(half, (q + 2) % SIDE, 0, 0, 1)
        hop2(half, (q + 2) % SIDE, 1, 1, 3)
        hop2(half, (q + 1) % SIDE, 1, 3, 1)
        hop2(half, (q + 3) % SIDE, 0, 5, 3)
    for half in range(2):
        q = place[1 - half]
        add2(half, (q + 1) % SIDE, 0, 0)
        hop2(half, (q + 1) % SIDE, 0, 2, 1)
        add2(half, (q + 3) % SIDE, 1, 1)
        hop2(half, (q + 3) % SIDE, 1, 4, 3)

    row_to, e = c // 2, c % 2
    handed = []
    for half in range(2):
        q = place[1 - half]
        for n in (3, 5, 2, 4):
            arrived(in2.at[half, n], p2_rsem.at[half, n])
        for piece, (m, n) in enumerate(((2, 5), (3, 4))):
            for b in range(QUART // AB):
                s = slice(b * AB, (b + 1) * AB)
                o = piece * QUART + b * AB
                keep = mask_ref[node, r * blocks + (half * HALF + o) // AB]
                value = tot[half, q, piece, :, s].astype(F32) + in2[half, m, :, s].astype(F32)
                value = value + in2[half, n, :, s].astype(F32)
                value = jnp.where(jnp.full((PB, AB), keep, jnp.int32) > 0, -value, 0.0).astype(BF16)
                upper_ref[:, half * HALF + o : half * HALF + o + AB] = value
                usend[half, :, o : o + AB] = value
        copy = send(
            usend.at[half], ubuf.at[e], u_ssem.at[half], u_rsem.at[e], row_to, 2 * r + half
        )
        mine = (row_to == r) & (e == half)

        @pl.when(mine)
        def _(half=half):
            ubuf[e] = usend[half]

        @pl.when(jnp.logical_not(mine))
        def _(copy=copy):
            copy.start()

        handed.append((copy, mine))

    for s in range(2):

        @pl.when(jnp.logical_not((row_to == r) & (e == s)))
        def _(s=s):
            arrived(ubuf.at[s], u_rsem.at[s])

    mine_k = r // 4

    def owner_part(i, _):
        rows = jnp.concatenate([ubuf[0], ubuf[1]], axis=0)
        value = lax.dot_general(
            rows, lm[mine_k * (W // PB) + i], (((1,), (1,)), ((), ())), preferred_element_type=F32
        )
        value = jnp.concatenate([value, jnp.zeros((2 * PB, AB - PB), F32)], axis=1).astype(BF16)
        for s in range(2):
            sendd[i, s] = value[s * PB : (s + 1) * PB]
            mine = (i == r) & (2 * r + s == c)

            @pl.when(mine)
            def _(s=s):
                recvd[c] = sendd[i, s]

            @pl.when(jnp.logical_not(mine))
            def _(s=s):
                send(
                    sendd.at[i, s], recvd.at[c], d_ssem.at[i, s], d_rsem.at[c], i, 2 * r + s
                ).start()

        return 0

    lax.fori_loop(0, W // PB, owner_part, 0)

    diag_ref[...] = dinv_ref[...]

    def collect(i, _):
        @pl.when(jnp.logical_not((row_to == r) & (i == c)))
        def _():
            arrived(recvd.at[i], d_rsem.at[i])

        diag_ref[...] = diag_ref[...] - recvd[i, :, :PB].astype(F32)
        return 0

    lax.fori_loop(0, SIDE * SIDE, collect, 0)

    for copy in started:
        copy.wait_send()
    for copy, mine in spread + handed:

        @pl.when(jnp.logical_not(mine))
        def _(copy=copy):
            copy.wait_send()

    def drain(n, _):
        b = nth(n, k)
        send(lm.at[b], lm.at[b], f_ssem.at[n], f_rsem.at[b], other, c).wait_send()
        for s in range(2):

            @pl.when(jnp.logical_not((n == r) & (2 * r + s == c)))
            def _(s=s):
                send(
                    sendd.at[n, s], recvd.at[c], d_ssem.at[n, s], d_rsem.at[c], n, 2 * r + s
                ).wait_send()

        return 0

    lax.fori_loop(0, 8, drain, 0)


def inverted(struct_mask, ainv_anc, l_panel, diag_inv):
    rows, width = l_panel.shape
    vmem, dma = pltpu.VMEM, pltpu.SemaphoreType.DMA
    spec = pl.BlockSpec(memory_space=pltpu.VMEM)
    return pl.pallas_call(
        invert_kernel,
        out_shape=(
            jax.ShapeDtypeStruct((rows, width), BF16),
            jax.ShapeDtypeStruct(diag_inv.shape, F32),
        ),
        in_specs=[
            pl.BlockSpec(memory_space=pltpu.SMEM),
            pl.BlockSpec(memory_space=pl.ANY),
            spec,
            spec,
        ],
        out_specs=(spec, spec),
        scratch_shapes=[
            vmem((SIDE, 2, PB, HALF), BF16),
            vmem((SIDE * SIDE, PB, HALF), BF16),
            vmem(ainv_anc.shape, BF16),
            vmem((2, 4, 2, SIDE * PB, QUART), BF16),
            vmem((2, 6, SIDE * PB, QUART), BF16),
            vmem((2, SIDE, 2, PB, QUART), BF16),
            vmem((2, 6, PB, QUART), BF16),
            vmem((2, PB, HALF), BF16),
            vmem((2, PB, HALF), BF16),
            vmem((8, 2, PB, AB), BF16),
            vmem((SIDE * SIDE, PB, AB), BF16),
            dma(()),
            dma((6,)), dma((6,)),
            dma((8,)), dma((16,)),
            dma((8,)), dma((16,)),
            dma((2, 6)), dma((2, 6)),
            dma((2, 6)), dma((2, 6)),
            dma((2,)), dma((2,)),
            dma((8, 2)), dma((16,)),
        ],
        compiler_params=pltpu.CompilerParams(
            has_side_effects=True, vmem_limit_bytes=52 * 1024 * 1024
        ),
        cost_estimate=pl.CostEstimate(
            flops=100_000_000_000, bytes_accessed=12_000_000, transcendentals=0
        ),
        name="invert",
    )(struct_mask, ainv_anc, l_panel, diag_inv)


def local(ainv_anc, l_panel, diag_inv, struct_mask, pieces, tile_owner):
    devices = lax.axis_size("row") * lax.axis_size("col")
    slots = packed(tile_owner[:, 0], pieces, devices)
    parts = slots.reshape(devices, SLOT, *pieces.shape[1:])
    arrived = lax.all_to_all(parts, ("row", "col"), split_axis=0, concat_axis=0, tiled=True)
    upper, diag = inverted(struct_mask, ainv_anc, l_panel, diag_inv)
    moved = arrived.astype(F32).reshape(slots.shape)
    return upper, diag, moved


def solution(mesh):
    in_specs = (
        P("row", "col"),
        P("col", "row"),
        P("col", "row"),
        P(),
        P(("row", "col"), None, None),
        P(("row", "col"), None),
    )
    out_specs = (P("col", "row"), P("col", "row"), P(("row", "col"), None, None))
    return jax.shard_map(local, mesh=mesh, in_specs=in_specs, out_specs=out_specs, check_vma=False)
```

time: 334 us -> 219 us (0.66)
  waiting for transfers between devices: 225 us -> 0.01 us
  Pallas kernels: 0 us -> 197 us
  local copies, waits for them, and re-layouts: 29.6 us -> 1.44 us
  matrix products: 24.2 us -> 0 us
  other arithmetic: 19.6 us -> 5.49 us
  between operations: 13.9 us -> 0.68 us
  starting transfers between devices: 16.7 us -> 11.1 us
    pallas_call x0 -> x2, Pallas kernels: none -> 197 us  [the longest x1 191 us: inverted(): pl.pallas_call(invert_kernel, out_shape=(jax.ShapeDtypeStruct((rows, widt...]
    all_gather x1 -> x0, waiting for transfers between devices: 76.8 us -> none  [local(): gathered = lax.all_gather(masked, 'col', axis=0, tiled=True)]
    psum x1 -> x0, waiting for transfers between devices: 74.1 us -> none  [broadcast(): return lax.psum(jnp.where(mine, value, jnp.zeros_like(value)), axis)]
    reduce_scatter x1 -> x0, waiting for transfers between devices: 72.3 us -> none  [local(): lax.psum_scatter(lax.dot_general(cross_rows, ainv_anc, (((1,), (1,)), (()...]
    dot_general x2 -> x0, matrix products: 24.2 us -> none  [the longest x1 20.3 us: local(): lax.dot_general(cross_rows, ainv_anc, (((1,), (1,)), ((), ())), preferred...]
    scatter x1 -> x0, local copies, waits for them, and re-layouts: 23.6 us -> none  [local(): buffer = jnp.zeros((devices_all * SLOT, piece_rows, piece_cols), jnp.floa...]
    convert_element_type x3 -> x0, other arithmetic: 10.4 us -> none  [the longest x1 5.37 us: local(): shaped.astype(jnp.bfloat16)]
    select_n x3 -> x0, other arithmetic: 7.27 us -> none  [the longest x1 5.33 us: broadcast(): return lax.psum(jnp.where(mine, value, jnp.zeros_like(value)), axis)]
  transfers between devices with their start and end apart: 5 -> 1, of which waited for: 4 -> 0; matrix products, arithmetic and copies ran while one was open for 13% -> 0% of each run, Pallas kernels for 0% -> 88%
where the time goes in v1:
time: 219 us; the launch traced here: 216 us
  Pallas kernels  197 us (90%)
  starting transfers between devices  11.1 us (5%)
  other arithmetic  5.49 us (3%)
    pallas_call x1, Pallas kernels, inverted(): pl.pallas_call(invert_kernel, out_shape=(jax.ShapeDtypeStruct((rows, widt...  191 us
    all_to_all x1, starting transfers between devices, local(): lax.all_to_all(parts, ('row', 'col'), split_axis=0, concat_axis=0, tiled=...  11.1 us
    pallas_call x1, Pallas kernels, packed(): pl.pallas_call(pack_kernel, out_shape=jax.ShapeDtypeStruct(shape, BF16),...  6.47 us
    reshape x1, other arithmetic, local(): moved = arrived.astype(F32).reshape(slots.shape)  5.49 us
  transfers between devices with their start and end apart: 1, of which 0 were waited for; matrix products, arithmetic and copies ran while one was open for 0% of the time, Pallas kernels for 88%

profile of v1, /device:TPU:13, one launch (start us, length us, event | category | flops | bytes accessed | tf_op | source)
XLA Modules:
  0.0 216.2 jit_solution(7518646378785192391)
XLA Ops:
  0.6 6.5 %pack.1 = bf16[384,32,128]{2,1,0:T(8,128)(2,1)} custom-call(s32[192]{0:T(256)} %bitcast.6, f32[192,32,128]{2,1,0:T(8,128)} %pieces_ref.1), custom_call_target="tpu_custom_call" | custom-call | tf_op jit(solution)/shard_map/pack/pallas_call | solution.py:46
  7.1 0.0 copy-start
  7.1 0.0 copy-start.1
  7.1 0.0 copy-start.2
  7.1 11.1 %all-to-all-start = ((bf16[128,3,32,128]{3,2,1,0:T(8,128)(2,1)}), bf16[128,3,32,128]{3,2,1,0:T(8,128)(2,1)}, u32[]{:S(2)}, u32[]{:S(2)}) async-start(bf16[128,3,32,128]{3,2,1,0:T(8,128)(2,1)} %bitcast.5), calls=%async_computation | async-start | bytes 6291456 | tf_op jit(solution)/shard_map/all_to_all | solution.py:414
  18.2 0.0 copy-done
  18.2 0.0 copy-done.1
  18.2 0.0 copy-done.2
  18.2 191.0 %invert.1 = (bf16[96,3072]{1,0:T(8,128)(2,1)S(1)}, f32[96,96]{1,0:T(8,128)S(1)}) custom-call(s32[2,192]{1,0:T(2,128)S(1)} %copy-done.2, bf16[3072,1536]{1,0:T(8,128)(2,1)} %a_hbm.1, bf16[96,3072]{1,0:T(8,128)(2,1)S(1)} %copy-done, f32[96,96]{1,0:T(8,128)S(1)} %copy-done.1), custom_call_target="tpu_custom_call" | custom-call | flops 99999997952 | bytes 12000000 | tf_op jit(solution)/shard_map/invert/pallas_call | solution.py:366
  209.2 0.0 all-to-all-done
  209.2 5.5 %bitcast_convert_fusion = f32[384,32,128]{2,1,0:T(8,128)} fusion(bf16[128,3,32,128]{3,2,1,0:T(8,128)(2,1)} %all-to-all-done), kind=kLoop, calls=%fused_computation | loop fusion | flops 1572864 | bytes 9437184 | tf_op jit(solution)/shard_map/reshape | solution.py:416
  214.7 0.8 copy.11
  215.5 0.6 copy.12
Async XLA Ops:
  7.1 11.1 %copy-start = (bf16[96,3072]{1,0:T(8,128)(2,1)S(1)}, bf16[96,3072]{1,0:T(8,128)(2,1)}, u32[]{:S(2)}) copy-start(bf16[96,3072]{1,0:T(8,128)(2,1)} %panel_ref.1) | copy-start | bytes 1769476
  7.1 11.1 %copy-start.1 = (f32[96,96]{1,0:T(8,128)S(1)}, f32[96,96]{1,0:T(8,128)}, u32[]{:S(2)}) copy-start(f32[96,96]{1,0:T(8,128)} %dinv_ref.1) | copy-start | bytes 110596
  7.1 11.1 %copy-start.2 = (s32[2,192]{1,0:T(2,128)S(1)}, s32[2,192]{1,0:T(2,128)}, u32[]{:S(2)}) copy-start(s32[2,192]{1,0:T(2,128)} %mask_ref.1) | copy-start | bytes 4612
  7.1 202.1 %all-to-all-start = ((bf16[128,3,32,128]{3,2,1,0:T(8,128)(2,1)}), bf16[128,3,32,128]{3,2,1,0:T(8,128)(2,1)}, u32[]{:S(2)}, u32[]{:S(2)}) async-start(bf16[128,3,32,128]{3,2,1,0:T(8,128)(2,1)} %bitcast.5), calls=%async_computation | async-start | bytes 6291456 | tf_op jit(solution)/shard_map/all_to_all | solution.py:414

commit v2 on v1

--- a/solution.py
+++ b/solution.py
@@ -10,6 +10,8 @@
 SLOT = 3
 SIDE = 4
 PB = 96
+SUBS, SUB = 6, 16
+AHEAD = 2
 HALF = 1536
 QUART = 768
 TILE = 256
@@ -58,13 +60,14 @@
 
 def invert_kernel(
     mask_ref, a_hbm, panel_ref, dinv_ref, upper_ref, diag_ref,
-    zbuf, lm, a, part, in1, tot, in2, usend, ubuf, sendd, recvd,
-    a_sem, z_ssem, z_rsem, l_ssem, l_rsem, f_ssem, f_rsem,
+    lmx, lm, a, part, in1, tot, in2, usend, ubuf, sendd, recvd,
+    a_sem, x_ssem, x_rsem, g_ssem, l_rsem, c_ssem, f_ssem, f_rsem,
     p1_ssem, p1_rsem, p2_ssem, p2_rsem, u_ssem, u_rsem, d_ssem, d_rsem,
 ):
     r, c = lax.axis_index("row"), lax.axis_index("col")
     z, k = r // 2, r % 2
     y, x = c // SIDE, c % SIDE
+    twin = y + 1 - 2 * (y % 2)
     node = c // (W // PB)
     started = []
 
@@ -88,85 +91,117 @@
     a_copy = pltpu.make_async_copy(a_hbm, a, a_sem)
     a_copy.start()
 
+    barrier = pltpu.get_barrier_semaphore()
+
+    def greet(row, col):
+        pl.semaphore_signal(
+            barrier, inc=1, device_id=at(row, col), device_id_type=pl.DeviceIdType.MESH
+        )
+
+    def greet_plane(n, _):
+        d = n // 2
+        greet(2 * z + (k + n) % 2, SIDE * ((y + d // SIDE) % SIDE) + (x + d) % SIDE)
+        return 0
+
+    def greet_z(n, _):
+        row = (2 * z + 2 + n) % (2 * SIDE)
+        greet(row, c)
+        greet(row, SIDE * twin + x)
+        return 0
+
+    lax.fori_loop(1, 2 * SIDE * SIDE, greet_plane, 0)
+    lax.fori_loop(0, 2 * SIDE - 2, greet_z, 0)
+
     blocks = panel_ref.shape[1] // AB
     for b in range(blocks):
         keep = jnp.full((PB, AB), mask_ref[node, r * blocks + b], jnp.int32) > 0
         value = panel_ref[:, b * AB : (b + 1) * AB].astype(F32)
         h, o = divmod(b * AB, HALF)
-        zbuf[z, h, :, o : o + AB] = jnp.where(keep, value, 0.0).astype(BF16)
-
-    zp, zm, zo = (z + 1) % SIDE, (z + 3) % SIDE, (z + 2) % SIDE
-    up, down = 2 * zp + k, 2 * zm + k
-    go(zbuf.at[z, 0], zbuf.at[z, 0], z_ssem.at[0], z_rsem.at[0], up, c)
-    go(zbuf.at[z, 1], zbuf.at[z, 1], z_ssem.at[1], z_rsem.at[1], down, c)
-    go(zbuf.at[z, 1], zbuf.at[z, 1], z_ssem.at[2], z_rsem.at[2], up, c)
-    go(zbuf.at[z, 0], zbuf.at[z, 0], z_ssem.at[3], z_rsem.at[3], down, c)
+        value = jnp.where(keep, value, 0.0).astype(BF16)
+        lmx[x, h, :, :, o : o + AB] = value.reshape(SUBS, SUB, AB)
+
+    pl.semaphore_wait(barrier, 2 * SIDE * SIDE - 1 + 2 * (2 * SIDE - 2))
 
     core = (x + y) % 2
-
-    def own_block(zs, h):
-        return (SIDE * zs + 2 * k + h == c) & (k == core)
-
-    spread = []
-
-    def to_column(n, zs, h):
-        copy = send(
-            zbuf.at[zs, h], lm.at[c], l_ssem.at[n], l_rsem.at[c],
-            2 * z + core, SIDE * zs + 2 * k + h,
-        )
-        mine = own_block(zs, h)
-
-        @pl.when(mine)
-        def _():
-            lm[c] = zbuf[zs, h]
-
-        @pl.when(jnp.logical_not(mine))
-        def _():
-            copy.start()
-
-        spread.append((copy, mine))
-
-    to_column(0, z, 0)
-    to_column(1, z, 1)
-    arrived(zbuf.at[zm, 0], z_rsem.at[0])
-    go(zbuf.at[zm, 0], zbuf.at[zm, 0], z_ssem.at[4], z_rsem.at[4], up, c)
-    arrived(zbuf.at[zp, 1], z_rsem.at[1])
-    go(zbuf.at[zp, 1], zbuf.at[zp, 1], z_ssem.at[5], z_rsem.at[5], down, c)
-    to_column(2, zm, 0)
-    to_column(3, zp, 1)
-    arrived(zbuf.at[zm, 1], z_rsem.at[2])
-    to_column(4, zm, 1)
-    arrived(zbuf.at[zp, 0], z_rsem.at[3])
-    to_column(5, zp, 0)
-    arrived(zbuf.at[zo, 0], z_rsem.at[4])
-    to_column(6, zo, 0)
-    arrived(zbuf.at[zo, 1], z_rsem.at[5])
-    to_column(7, zo, 1)
+    root_row = 2 * z + core
+
+    def own_block(h):
+        return (SIDE * z + 2 * k + h == c) & (k == core)
+
+    def gather(s, wait):
+        for h in range(2):
+            copy = send(
+                lmx.at[x, h, s], lm.at[c, s], g_ssem.at[h, s], l_rsem.at[c, s],
+                root_row, SIDE * z + 2 * k + h,
+            )
+            mine = own_block(h)
+
+            @pl.when(jnp.logical_not(mine))
+            def _(copy=copy):
+                copy.wait_send() if wait else copy.start()
+
+            if not wait:
+
+                @pl.when(mine)
+                def _(h=h):
+                    lm[c, s] = lmx[x, h, s]
+
+    for s in range(AHEAD):
+        gather(s, False)
+
+    xp, xm, xo = (x + 1) % SIDE, (x + 3) % SIDE, (x + 2) % SIDE
+    right, left = SIDE * y + xp, SIDE * y + xm
+    go(lmx.at[x, 0], lmx.at[x, 0], x_ssem.at[0], x_rsem.at[0], r, right)
+    go(lmx.at[x, 1], lmx.at[x, 1], x_ssem.at[1], x_rsem.at[1], r, left)
+    go(lmx.at[x, 1], lmx.at[x, 1], x_ssem.at[2], x_rsem.at[2], r, right)
+    go(lmx.at[x, 0], lmx.at[x, 0], x_ssem.at[3], x_rsem.at[3], r, left)
 
     other = 2 * z + 1 - k
+    following = 2 * ((z + 1 + 2 * k) % SIDE) + k
+    first, last = z == y, following // 2 == y
 
     def nth(n, parity):
         yy, xx = n // 2, n % 2
         return SIDE * yy + 2 * xx + (yy + parity) % 2
 
-    def hand_on(n, _):
+    def hand_on(i, _):
+        n, s = i % 8, i // 8
         b = nth(n, k)
 
-        @pl.when(jnp.logical_not((b == c) & (x // 2 == k)))
+        @pl.when(jnp.logical_not(first & (b == c) & (x // 2 == k)))
         def _():
-            arrived(lm.at[b], l_rsem.at[b])
-
-        send(lm.at[b], lm.at[b], f_ssem.at[n], f_rsem.at[b], other, c).start()
-        return 0
-
-    lax.fori_loop(0, 8, hand_on, 0)
-
-    def take(n, _):
-        b = nth(n, 1 - k)
-        arrived(lm.at[b], f_rsem.at[b])
-        return 0
-
-    lax.fori_loop(0, 8, take, 0)
+            arrived(lm.at[b, s], l_rsem.at[b, s])
+
+        @pl.when(jnp.logical_not(last))
+        def _():
+            send(lm.at[b, s], lm.at[b, s], c_ssem.at[n, s], l_rsem.at[b, s], following, c).start()
+
+        send(lm.at[b, s], lm.at[b, s], f_ssem.at[n, s], f_rsem.at[b, s], other, c).start()
+        return 0
+
+    def part_on(s, _):
+        gather(s, True)
+
+        @pl.when(s + AHEAD < SUBS)
+        def _():
+            gather(s + AHEAD, False)
+
+        return lax.fori_loop(8 * s, 8 * s + 8, hand_on, 0)
+
+    lax.fori_loop(0, SUBS // 2, part_on, 0)
+    arrived(lmx.at[xm, 0], x_rsem.at[0])
+    go(lmx.at[xm, 0], lmx.at[xm, 0], x_ssem.at[4], x_rsem.at[4], r, right)
+    arrived(lmx.at[xp, 1], x_rsem.at[1])
+    go(lmx.at[xp, 1], lmx.at[xp, 1], x_ssem.at[5], x_rsem.at[5], r, left)
+    lax.fori_loop(SUBS // 2, SUBS, part_on, 0)
+
+    def take(i, _):
+        s = i // 8
+        b = nth(i % 8, 1 - k)
+        arrived(lm.at[b, s], f_rsem.at[b, s])
+        return 0
+
+    lax.fori_loop(0, 8 * SUBS, take, 0)
     a_copy.wait()
 
     place = (x, y)
@@ -182,7 +217,9 @@
         across, along = (SIDE, 1) if half == 0 else (1, SIDE)
 
         def tile(t, _):
-            rows = jnp.concatenate([lm[j * across + dest * along] for j in range(SIDE)], axis=0)
+            rows = jnp.concatenate(
+                [lm[j * across + dest * along].reshape(PB, HALF) for j in range(SIDE)], axis=0
+            )
             cols = a[pl.ds(pl.multiple_of(half * HALF + t * TILE, TILE), TILE), :]
             value = lax.dot_general(rows, cols, (((1,), (1,)), ((), ())), preferred_element_type=F32)
             per = QUART // TILE
@@ -260,8 +297,6 @@
         add2(half, (q + 3) % SIDE, 1, 1)
         hop2(half, (q + 3) % SIDE, 1, 4, 3)
 
-    row_to, e = c // 2, c % 2
-    handed = []
     for half in range(2):
         q = place[1 - half]
         for n in (3, 5, 2, 4):
@@ -276,87 +311,92 @@
                 value = jnp.where(jnp.full((PB, AB), keep, jnp.int32) > 0, -value, 0.0).astype(BF16)
                 upper_ref[:, half * HALF + o : half * HALF + o + AB] = value
                 usend[half, :, o : o + AB] = value
-        copy = send(
-            usend.at[half], ubuf.at[e], u_ssem.at[half], u_rsem.at[e], row_to, 2 * r + half
-        )
-        mine = (row_to == r) & (e == half)
-
-        @pl.when(mine)
-        def _(half=half):
-            ubuf[e] = usend[half]
-
-        @pl.when(jnp.logical_not(mine))
-        def _(copy=copy):
-            copy.start()
-
-        handed.append((copy, mine))
-
-    for s in range(2):
-
-        @pl.when(jnp.logical_not((row_to == r) & (e == s)))
-        def _(s=s):
-            arrived(ubuf.at[s], u_rsem.at[s])
-
-    mine_k = r // 4
-
-    def owner_part(i, _):
-        rows = jnp.concatenate([ubuf[0], ubuf[1]], axis=0)
-        value = lax.dot_general(
-            rows, lm[mine_k * (W // PB) + i], (((1,), (1,)), ((), ())), preferred_element_type=F32
-        )
-        value = jnp.concatenate([value, jnp.zeros((2 * PB, AB - PB), F32)], axis=1).astype(BF16)
-        for s in range(2):
-            sendd[i, s] = value[s * PB : (s + 1) * PB]
-            mine = (i == r) & (2 * r + s == c)
-
-            @pl.when(mine)
-            def _(s=s):
-                recvd[c] = sendd[i, s]
-
-            @pl.when(jnp.logical_not(mine))
-            def _(s=s):
-                send(
-                    sendd.at[i, s], recvd.at[c], d_ssem.at[i, s], d_rsem.at[c], i, 2 * r + s
-                ).start()
-
-        return 0
-
-    lax.fori_loop(0, W // PB, owner_part, 0)
+        go(usend.at[half], ubuf.at[half], u_ssem.at[half], u_rsem.at[half], r, SIDE * twin + x)
+
+    for n, (b, h) in enumerate(((xm, 1), (xp, 0), (xo, 0), (xo, 1))):
+        arrived(lmx.at[b, h], x_rsem.at[2 + n])
+
+    owner0 = (y % 2) * SIDE
+
+    def partial(s, source):
+        def one(i, _):
+            value = jnp.zeros((PB, PB), F32)
+            for h in range(2):
+                value = value + lax.dot_general(
+                    source[h], lmx[i, h].reshape(PB, HALF), (((1,), (1,)), ((), ())),
+                    preferred_element_type=F32,
+                )
+            sendd[s, i, :, :PB] = value.astype(BF16)
+            copy = send(
+                sendd.at[s, i], recvd.at[r], d_ssem.at[s, i], d_rsem.at[r],
+                owner0 + i, SIDE * (y, twin)[s] + x,
+            )
+            if s:
+                copy.start()
+            else:
+
+                @pl.when(owner0 + i == r)
+                def _():
+                    recvd[r] = sendd[s, i]
+
+                @pl.when(owner0 + i != r)
+                def _():
+                    copy.start()
+
+            return 0
+
+        lax.fori_loop(0, SIDE, one, 0)
+
+    sendd[...] = jnp.zeros_like(sendd)
+    partial(0, usend)
+    for h in range(2):
+        arrived(ubuf.at[h], u_rsem.at[h])
+    partial(1, ubuf)
 
     diag_ref[...] = dinv_ref[...]
 
     def collect(i, _):
-        @pl.when(jnp.logical_not((row_to == r) & (i == c)))
+        @pl.when(jnp.logical_not((i == r) & (r // SIDE == y % 2)))
         def _():
             arrived(recvd.at[i], d_rsem.at[i])
 
         diag_ref[...] = diag_ref[...] - recvd[i, :, :PB].astype(F32)
         return 0
 
-    lax.fori_loop(0, SIDE * SIDE, collect, 0)
+    lax.fori_loop(0, 2 * SIDE, collect, 0)
 
     for copy in started:
         copy.wait_send()
-    for copy, mine in spread + handed:
-
-        @pl.when(jnp.logical_not(mine))
-        def _(copy=copy):
-            copy.wait_send()
-
-    def drain(n, _):
+    def drain(i, _):
+        n, s = i % 8, i // 8
         b = nth(n, k)
-        send(lm.at[b], lm.at[b], f_ssem.at[n], f_rsem.at[b], other, c).wait_send()
+
+        @pl.when(jnp.logical_not(last))
+        def _():
+            send(lm.at[b, s], lm.at[b, s], c_ssem.at[n, s], l_rsem.at[b, s], following, c).wait_send()
+
+        send(lm.at[b, s], lm.at[b, s], f_ssem.at[n, s], f_rsem.at[b, s], other, c).wait_send()
+        return 0
+
+    lax.fori_loop(0, 8 * SUBS, drain, 0)
+
+    def drain_diag(i, _):
         for s in range(2):
-
-            @pl.when(jnp.logical_not((n == r) & (2 * r + s == c)))
-            def _(s=s):
-                send(
-                    sendd.at[n, s], recvd.at[c], d_ssem.at[n, s], d_rsem.at[c], n, 2 * r + s
-                ).wait_send()
-
-        return 0
-
-    lax.fori_loop(0, 8, drain, 0)
+            copy = send(
+                sendd.at[s, i], recvd.at[r], d_ssem.at[s, i], d_rsem.at[r],
+                owner0 + i, SIDE * (y, twin)[s] + x,
+            )
+            if s:
+                copy.wait_send()
+            else:
+
+                @pl.when(owner0 + i != r)
+                def _(copy=copy):
+                    copy.wait_send()
+
+        return 0
+
+    lax.fori_loop(0, SIDE, drain_diag, 0)
 
 
 def inverted(struct_mask, ainv_anc, l_panel, diag_inv):
@@ -377,8 +417,8 @@
         ],
         out_specs=(spec, spec),
         scratch_shapes=[
-            vmem((SIDE, 2, PB, HALF), BF16),
-            vmem((SIDE * SIDE, PB, HALF), BF16),
+            vmem((SIDE, 2, SUBS, SUB, HALF), BF16),
+            vmem((SIDE * SIDE, SUBS, SUB, HALF), BF16),
             vmem(ainv_anc.shape, BF16),
             vmem((2, 4, 2, SIDE * PB, QUART), BF16),
             vmem((2, 6, SIDE * PB, QUART), BF16),
@@ -386,19 +426,19 @@
             vmem((2, 6, PB, QUART), BF16),
             vmem((2, PB, HALF), BF16),
             vmem((2, PB, HALF), BF16),
-            vmem((8, 2, PB, AB), BF16),
-            vmem((SIDE * SIDE, PB, AB), BF16),
+            vmem((2, SIDE, PB, AB), BF16),
+            vmem((2 * SIDE, PB, AB), BF16),
             dma(()),
             dma((6,)), dma((6,)),
-            dma((8,)), dma((16,)),
-            dma((8,)), dma((16,)),
+            dma((2, SUBS)), dma((16, SUBS)),
+            dma((8, SUBS)), dma((8, SUBS)), dma((16, SUBS)),
             dma((2, 6)), dma((2, 6)),
             dma((2, 6)), dma((2, 6)),
             dma((2,)), dma((2,)),
-            dma((8, 2)), dma((16,)),
+            dma((2, SIDE)), dma((2 * SIDE,)),
         ],
         compiler_params=pltpu.CompilerParams(
-            has_side_effects=True, vmem_limit_bytes=52 * 1024 * 1024
+            collective_id=0, has_side_effects=True, vmem_limit_bytes=52 * 1024 * 1024
         ),
         cost_estimate=pl.CostEstimate(
             flops=100_000_000_000, bytes_accessed=12_000_000, transcendentals=0

time: 219 us -> 195 us (0.89)
  Pallas kernels: 197 us -> 173 us
    pallas_call x1, Pallas kernels: 191 us -> 166 us  [inverted(): pl.pallas_call(invert_kernel, out_shape=(jax.ShapeDtypeStruct((rows, widt...]
  transfers between devices with their start and end apart: 1 -> 1, of which waited for: 0 -> 0; matrix products, arithmetic and copies ran while one was open for 0% -> 0% of each run, Pallas kernels for 88% -> 87%
where the time goes in v2:
time: 195 us; the launch traced here: 192 us
  Pallas kernels  173 us (89%)
  starting transfers between devices  11.1 us (6%)
  other arithmetic  5.49 us (3%)
    pallas_call x1, Pallas kernels, inverted(): pl.pallas_call(invert_kernel, out_shape=(jax.ShapeDtypeStruct((rows, widt...  166 us
    all_to_all x1, starting transfers between devices, local(): lax.all_to_all(parts, ('row', 'col'), split_axis=0, concat_axis=0, tiled=...  11.1 us
    pallas_call x1, Pallas kernels, packed(): pl.pallas_call(pack_kernel, out_shape=jax.ShapeDtypeStruct(shape, BF16),...  6.47 us
    reshape x1, other arithmetic, local(): moved = arrived.astype(F32).reshape(slots.shape)  5.49 us
  transfers between devices with their start and end apart: 1, of which 0 were waited for; matrix products, arithmetic and copies ran while one was open for 0% of the time, Pallas kernels for 87%

profile of v2, /device:TPU:13, one launch (start us, length us, event | category | flops | bytes accessed | tf_op | source)
XLA Modules:
  0.0 191.6 jit_solution(9086956357227076548)
XLA Ops:
  0.6 6.5 %pack.1 = bf16[384,32,128]{2,1,0:T(8,128)(2,1)} custom-call(s32[192]{0:T(256)} %bitcast.6, f32[192,32,128]{2,1,0:T(8,128)} %pieces_ref.1), custom_call_target="tpu_custom_call" | custom-call | tf_op jit(solution)/shard_map/pack/pallas_call | solution.py:48
  7.1 0.0 copy-start
  7.1 0.0 copy-start.1
  7.1 0.0 copy-start.2
  7.1 11.1 %all-to-all-start = ((bf16[128,3,32,128]{3,2,1,0:T(8,128)(2,1)}), bf16[128,3,32,128]{3,2,1,0:T(8,128)(2,1)}, u32[]{:S(2)}, u32[]{:S(2)}) async-start(bf16[128,3,32,128]{3,2,1,0:T(8,128)(2,1)} %bitcast.5), calls=%async_computation | async-start | bytes 6291456 | tf_op jit(solution)/shard_map/all_to_all | solution.py:454
  18.2 0.0 copy-done
  18.2 0.0 copy-done.1
  18.2 0.0 copy-done.2
  18.2 166.5 %invert.1 = (bf16[96,3072]{1,0:T(8,128)(2,1)S(1)}, f32[96,96]{1,0:T(8,128)S(1)}) custom-call(s32[2,192]{1,0:T(2,128)S(1)} %copy-done.2, bf16[3072,1536]{1,0:T(8,128)(2,1)} %a_hbm.1, bf16[96,3072]{1,0:T(8,128)(2,1)S(1)} %copy-done, f32[96,96]{1,0:T(8,128)S(1)} %copy-done.1), custom_call_target="tpu_custom_call" | custom-call | flops 99999997952 | bytes 12000000 | tf_op jit(solution)/shard_map/invert/pallas_call | solution.py:406
  184.7 0.0 all-to-all-done
  184.7 5.5 %bitcast_convert_fusion = f32[384,32,128]{2,1,0:T(8,128)} fusion(bf16[128,3,32,128]{3,2,1,0:T(8,128)(2,1)} %all-to-all-done), kind=kLoop, calls=%fused_computation | loop fusion | flops 1572864 | bytes 9437184 | tf_op jit(solution)/shard_map/reshape | solution.py:456
  190.2 0.8 copy.11
  191.0 0.6 copy.12
Async XLA Ops:
  7.1 11.1 %copy-start = (bf16[96,3072]{1,0:T(8,128)(2,1)S(1)}, bf16[96,3072]{1,0:T(8,128)(2,1)}, u32[]{:S(2)}) copy-start(bf16[96,3072]{1,0:T(8,128)(2,1)} %panel_ref.1) | copy-start | bytes 1769476
  7.1 11.1 %copy-start.1 = (f32[96,96]{1,0:T(8,128)S(1)}, f32[96,96]{1,0:T(8,128)}, u32[]{:S(2)}) copy-start(f32[96,96]{1,0:T(8,128)} %dinv_ref.1) | copy-start | bytes 110596
  7.1 11.1 %copy-start.2 = (s32[2,192]{1,0:T(2,128)S(1)}, s32[2,192]{1,0:T(2,128)}, u32[]{:S(2)}) copy-start(s32[2,192]{1,0:T(2,128)} %mask_ref.1) | copy-start | bytes 4612
  7.1 177.6 %all-to-all-start = ((bf16[128,3,32,128]{3,2,1,0:T(8,128)(2,1)}), bf16[128,3,32,128]{3,2,1,0:T(8,128)(2,1)}, u32[]{:S(2)}, u32[]{:S(2)}) async-start(bf16[128,3,32,128]{3,2,1,0:T(8,128)(2,1)} %bitcast.5), calls=%async_computation | async-start | bytes 6291456 | tf_op jit(solution)/shard_map/all_to_all | solution.py:454

commit v3 on v2

--- a/solution.py
+++ b/solution.py
@@ -10,50 +10,73 @@
 SLOT = 3
 SIDE = 4
 PB = 96
-SUBS, SUB = 6, 16
-AHEAD = 2
+SUBS, SUB = 3, 32
+EVEN = ((2, 0), (2, 2), (0, 2), (0, 0), (1, 1), (1, 3), (3, 1), (3, 3))
+ODD = ((2, 1), (2, 3), (1, 2), (3, 2), (1, 0), (3, 0), (0, 1), (0, 3))
 HALF = 1536
 QUART = 768
 TILE = 256
 BF16, F32 = jnp.bfloat16, jnp.float32
 
 
-def pack_kernel(owner_ref, pieces_ref, out_ref, count_ref):
-    devices = out_ref.shape[0] // SLOT
-
-    def clear(i, _):
-        out_ref[pl.ds(i * 8, 8)] = jnp.zeros((8, *out_ref.shape[1:]), out_ref.dtype)
-        return 0
-
-    lax.fori_loop(0, out_ref.shape[0] // 8, clear, 0)
+def pack_kernel(owner_ref, pieces_hbm, out_ref, pieces, count_ref, slot_ref, sems):
+    parts = pieces.shape[0]
+    per = pieces.shape[1]
+    copies = [
+        pltpu.make_async_copy(pieces_hbm.at[pl.ds(i * per, per)], pieces.at[i], sems.at[i])
+        for i in range(parts)
+    ]
+    for copy in copies:
+        copy.start()
 
     def reset(i, _):
         count_ref[i] = 0
         return 0
 
-    lax.fori_loop(0, devices, reset, 0)
-
-    def place(p, _):
+    lax.fori_loop(0, out_ref.shape[0] // SLOT, reset, 0, unroll=8)
+
+    def number(p, _):
         owner = owner_ref[p]
         rank = count_ref[owner]
         count_ref[owner] = rank + 1
-        out_ref[owner * SLOT + rank] = pieces_ref[p].astype(out_ref.dtype)
-        return 0
-
-    lax.fori_loop(0, pieces_ref.shape[0], place, 0)
+        slot_ref[p] = owner * SLOT + rank
+        return 0
+
+    lax.fori_loop(0, parts * per, number, 0, unroll=4)
+
+    def clear(i, _):
+        out_ref[pl.ds(i * 16, 16)] = jnp.zeros((16, *out_ref.shape[1:]), out_ref.dtype)
+        return 0
+
+    lax.fori_loop(0, out_ref.shape[0] // 16, clear, 0)
+
+    for i in range(parts):
+        copies[i].wait()
+
+        def place(p, _, i=i):
+            out_ref[slot_ref[i * per + p]] = pieces[i, p].astype(out_ref.dtype)
+            return 0
+
+        lax.fori_loop(0, per, place, 0, unroll=8)
 
 
 def packed(owners, pieces, devices):
-    shape = (devices * SLOT, *pieces.shape[1:])
+    count, *inside = pieces.shape
+    parts = 4
     return pl.pallas_call(
         pack_kernel,
-        out_shape=jax.ShapeDtypeStruct(shape, BF16),
+        out_shape=jax.ShapeDtypeStruct((devices * SLOT, *inside), BF16),
         in_specs=[
             pl.BlockSpec(memory_space=pltpu.SMEM),
-            pl.BlockSpec(memory_space=pltpu.VMEM),
+            pl.BlockSpec(memory_space=pl.ANY),
         ],
         out_specs=pl.BlockSpec(memory_space=pltpu.VMEM),
-        scratch_shapes=[pltpu.SMEM((devices,), jnp.int32)],
+        scratch_shapes=[
+            pltpu.VMEM((parts, count // parts, *inside), pieces.dtype),
+            pltpu.SMEM((devices,), jnp.int32),
+            pltpu.SMEM((count,), jnp.int32),
+            pltpu.SemaphoreType.DMA((parts,)),
+        ],
         name="pack",
     )(owners, pieces)
 
@@ -128,80 +151,112 @@
     def own_block(h):
         return (SIDE * z + 2 * k + h == c) & (k == core)
 
-    def gather(s, wait):
-        for h in range(2):
-            copy = send(
+    def gather(h):
+        return [
+            send(
                 lmx.at[x, h, s], lm.at[c, s], g_ssem.at[h, s], l_rsem.at[c, s],
                 root_row, SIDE * z + 2 * k + h,
             )
-            mine = own_block(h)
-
-            @pl.when(jnp.logical_not(mine))
-            def _(copy=copy):
-                copy.wait_send() if wait else copy.start()
-
-            if not wait:
-
-                @pl.when(mine)
-                def _(h=h):
-                    lm[c, s] = lmx[x, h, s]
-
-    for s in range(AHEAD):
-        gather(s, False)
+            for s in range(SUBS)
+        ]
+
+    def soon(h):
+        far_x = (x + SIDE - 2 * k - h) % SIDE == 2
+        far_y = (y + SIDE - z) % SIDE == 2
+        return far_x | far_y | (y == z)
+
+    for h in range(2):
+
+        @pl.when(own_block(h))
+        def _(h=h):
+            for s in range(SUBS):
+                lm[c, s] = lmx[x, h, s]
+
+        @pl.when(soon(h) & jnp.logical_not(own_block(h)))
+        def _(h=h):
+            for copy in gather(h):
+                copy.start()
 
     xp, xm, xo = (x + 1) % SIDE, (x + 3) % SIDE, (x + 2) % SIDE
     right, left = SIDE * y + xp, SIDE * y + xm
     go(lmx.at[x, 0], lmx.at[x, 0], x_ssem.at[0], x_rsem.at[0], r, right)
     go(lmx.at[x, 1], lmx.at[x, 1], x_ssem.at[1], x_rsem.at[1], r, left)
-    go(lmx.at[x, 1], lmx.at[x, 1], x_ssem.at[2], x_rsem.at[2], r, right)
-    go(lmx.at[x, 0], lmx.at[x, 0], x_ssem.at[3], x_rsem.at[3], r, left)
+    passed_on = (
+        send(lmx.at[xm, 0], lmx.at[xm, 0], x_ssem.at[4], x_rsem.at[4], r, right),
+        send(lmx.at[xp, 1], lmx.at[xp, 1], x_ssem.at[5], x_rsem.at[5], r, left),
+    )
+    started.extend(passed_on)
+
+    def pass_on():
+        arrived(lmx.at[xm, 0], x_rsem.at[0])
+        passed_on[0].start()
+        arrived(lmx.at[xp, 1], x_rsem.at[1])
+        passed_on[1].start()
+
+    @pl.when(y != z)
+    def _():
+        pass_on()
+        for h in range(2):
+
+            @pl.when(jnp.logical_not(soon(h)))
+            def _(h=h):
+                for copy in gather(h):
+                    copy.start()
 
     other = 2 * z + 1 - k
     following = 2 * ((z + 1 + 2 * k) % SIDE) + k
     first, last = z == y, following // 2 == y
 
-    def nth(n, parity):
-        yy, xx = n // 2, n % 2
-        return SIDE * yy + 2 * xx + (yy + parity) % 2
-
-    def hand_on(i, _):
-        n, s = i % 8, i // 8
-        b = nth(n, k)
+    def nth(n, mine):
+        odd = (x + y + k + 1 - mine) % 2
+        dx = EVEN[n][0] + odd * (ODD[n][0] - EVEN[n][0])
+        dy = EVEN[n][1] + odd * (ODD[n][1] - EVEN[n][1])
+        return SIDE * ((y + dy) % SIDE) + (x + dx) % SIDE
+
+    def onward(n, s):
+        b = nth(n, 1)
+        return (
+            send(lm.at[b, s], lm.at[b, s], c_ssem.at[n, s], l_rsem.at[b, s], following, c),
+            send(lm.at[b, s], lm.at[b, s], f_ssem.at[n, s], f_rsem.at[b, s], other, c),
+        )
+
+    def hand_on(n, s):
+        b = nth(n, 1)
 
         @pl.when(jnp.logical_not(first & (b == c) & (x // 2 == k)))
         def _():
             arrived(lm.at[b, s], l_rsem.at[b, s])
 
+        chain, across = onward(n, s)
+
         @pl.when(jnp.logical_not(last))
         def _():
-            send(lm.at[b, s], lm.at[b, s], c_ssem.at[n, s], l_rsem.at[b, s], following, c).start()
-
-        send(lm.at[b, s], lm.at[b, s], f_ssem.at[n, s], f_rsem.at[b, s], other, c).start()
-        return 0
-
-    def part_on(s, _):
-        gather(s, True)
-
-        @pl.when(s + AHEAD < SUBS)
-        def _():
-            gather(s + AHEAD, False)
-
-        return lax.fori_loop(8 * s, 8 * s + 8, hand_on, 0)
-
-    lax.fori_loop(0, SUBS // 2, part_on, 0)
-    arrived(lmx.at[xm, 0], x_rsem.at[0])
-    go(lmx.at[xm, 0], lmx.at[xm, 0], x_ssem.at[4], x_rsem.at[4], r, right)
-    arrived(lmx.at[xp, 1], x_rsem.at[1])
-    go(lmx.at[xp, 1], lmx.at[xp, 1], x_ssem.at[5], x_rsem.at[5], r, left)
-    lax.fori_loop(SUBS // 2, SUBS, part_on, 0)
-
-    def take(i, _):
-        s = i // 8
-        b = nth(i % 8, 1 - k)
+            chain.start()
+
+        across.start()
+
+    def every_part(n, act):
+        def one(s, _):
+            act(n, s)
+            return 0
+
+        lax.fori_loop(0, SUBS, one, 0)
+
+    def take(n, s):
+        b = nth(n, 0)
         arrived(lm.at[b, s], f_rsem.at[b, s])
-        return 0
-
-    lax.fori_loop(0, 8 * SUBS, take, 0)
+
+    for n in range(4):
+        every_part(n, hand_on)
+
+    @pl.when(y == z)
+    def _():
+        pass_on()
+
+    go(lmx.at[x, 1], lmx.at[x, 1], x_ssem.at[2], x_rsem.at[2], r, right)
+    go(lmx.at[x, 0], lmx.at[x, 0], x_ssem.at[3], x_rsem.at[3], r, left)
+    for n in range(4):
+        every_part(n, take)
     a_copy.wait()
 
     place = (x, y)
@@ -213,7 +268,7 @@
 
     FAR, NEXT, LAST, OWN = range(4)
 
-    def multiply(half, slot, dest):
+    def multiply(half, slot, dest, blocks_due=()):
         across, along = (SIDE, 1) if half == 0 else (1, SIDE)
 
         def tile(t, _):
@@ -226,7 +281,16 @@
             part[half, slot, t // per, :, pl.ds(pl.multiple_of((t % per) * TILE, TILE), TILE)] = value.astype(BF16)
             return 0
 
-        lax.fori_loop(0, HALF // TILE, tile, 0)
+        if not blocks_due:
+            lax.fori_loop(0, HALF // TILE, tile, 0)
+        for i, n in enumerate(blocks_due):
+
+            def tile_and_part(s, _, i=i, n=n):
+                tile(SUBS * i + s, 0)
+                hand_on(n, s)
+                return 0
+
+            lax.fori_loop(0, SUBS, tile_and_part, 0)
 
     def hop1(half, slot, piece, n, step):
         go(
@@ -246,9 +310,11 @@
         lax.fori_loop(0, SIDE * PB // 32, rows, 0)
 
     for half in range(2):
-        multiply(half, FAR, (place[half] + 2) % SIDE)
+        multiply(half, FAR, (place[half] + 2) % SIDE, (4 + 2 * half, 5 + 2 * half))
         hop1(half, FAR, 0, 0, 1)
         hop1(half, FAR, 1, 1, 3)
+    for n in range(4, 8):
+        every_part(n, take)
     for half in range(2):
         multiply(half, NEXT, (place[half] + 1) % SIDE)
         hop1(half, NEXT, 1, 3, 1)
@@ -367,18 +433,24 @@
 
     for copy in started:
         copy.wait_send()
-    def drain(i, _):
-        n, s = i % 8, i // 8
-        b = nth(n, k)
+    for h in range(2):
+
+        @pl.when(jnp.logical_not(own_block(h)))
+        def _(h=h):
+            for copy in gather(h):
+                copy.wait_send()
+
+    def drain(n, s):
+        chain, across = onward(n, s)
 
         @pl.when(jnp.logical_not(last))
         def _():
-            send(lm.at[b, s], lm.at[b, s], c_ssem.at[n, s], l_rsem.at[b, s], following, c).wait_send()
-
-        send(lm.at[b, s], lm.at[b, s], f_ssem.at[n, s], f_rsem.at[b, s], other, c).wait_send()
-        return 0
-
-    lax.fori_loop(0, 8 * SUBS, drain, 0)
+            chain.wait_send()
+
+        across.wait_send()
+
+    for n in range(8):
+        every_part(n, drain)
 
     def drain_diag(i, _):
         for s in range(2):
@@ -438,7 +510,7 @@
             dma((2, SIDE)), dma((2 * SIDE,)),
         ],
         compiler_params=pltpu.CompilerParams(
-            collective_id=0, has_side_effects=True, vmem_limit_bytes=52 * 1024 * 1024
+            collective_id=0, has_side_effects=True, vmem_limit_bytes=44 * 1024 * 1024
         ),
         cost_estimate=pl.CostEstimate(
             flops=100_000_000_000, bytes_accessed=12_000_000, transcendentals=0

time: 195 us -> 182 us (0.933); the launches traced: 192 us -> 182 us
  Pallas kernels: 173 us -> 163 us
    pallas_call x1, Pallas kernels: 166 us -> 159 us  [inverted(): pl.pallas_call(invert_kernel, out_shape=(jax.ShapeDtypeStruct((rows, widt...]
    pallas_call x1, Pallas kernels: 6.47 us -> 4.4 us  [packed(): pl.pallas_call(pack_kernel, out_shape=jax.ShapeDtypeStruct((devices * SLO...]
where the time goes in v3:
time: 182 us
  Pallas kernels  163 us (90%)
  starting transfers between devices  11.1 us (6%)
  other arithmetic  5.49 us (3%)
    pallas_call x1, Pallas kernels, inverted(): pl.pallas_call(invert_kernel, out_shape=(jax.ShapeDtypeStruct((rows, widt...  159 us
    all_to_all x1, starting transfers between devices, local(): lax.all_to_all(parts, ('row', 'col'), split_axis=0, concat_axis=0, tiled=...  11.1 us
    reshape x1, other arithmetic, local(): moved = arrived.astype(F32).reshape(slots.shape)  5.49 us
    pallas_call x1, Pallas kernels, packed(): pl.pallas_call(pack_kernel, out_shape=jax.ShapeDtypeStruct((devices * SLO...  4.4 us
  transfers between devices with their start and end apart: 1, of which 0 were waited for; matrix products, arithmetic and copies ran while one was open for 0% of the time, Pallas kernels for 87%

profile of v3, /device:TPU:13, one launch (start us, length us, event | category | flops | bytes accessed | tf_op | source)
XLA Modules:
  0.0 181.7 jit_solution(10890299150737410210)
XLA Ops:
  0.6 4.4 %pack.1 = bf16[384,32,128]{2,1,0:T(8,128)(2,1)} custom-call(s32[192]{0:T(256)} %bitcast.6, f32[192,32,128]{2,1,0:T(8,128)} %pieces_hbm.1), custom_call_target="tpu_custom_call" | custom-call | tf_op jit(solution)/shard_map/pack/pallas_call | solution.py:66
  5.0 0.0 copy-start
  5.0 0.0 copy-start.1
  5.1 0.0 copy-start.2
  5.1 11.1 %all-to-all-start = ((bf16[128,3,32,128]{3,2,1,0:T(8,128)(2,1)}), bf16[128,3,32,128]{3,2,1,0:T(8,128)(2,1)}, u32[]{:S(2)}, u32[]{:S(2)}) async-start(bf16[128,3,32,128]{3,2,1,0:T(8,128)(2,1)} %bitcast.5), calls=%async_computation | async-start | bytes 6291456 | tf_op jit(solution)/shard_map/all_to_all | solution.py:526
  16.2 0.0 copy-done
  16.2 0.0 copy-done.1
  16.2 0.0 copy-done.2
  16.2 158.6 %invert.1 = (bf16[96,3072]{1,0:T(8,128)(2,1)S(1)}, f32[96,96]{1,0:T(8,128)S(1)}) custom-call(s32[2,192]{1,0:T(2,128)S(1)} %copy-done.2, bf16[3072,1536]{1,0:T(8,128)(2,1)} %a_hbm.1, bf16[96,3072]{1,0:T(8,128)(2,1)S(1)} %copy-done, f32[96,96]{1,0:T(8,128)S(1)} %copy-done.1), custom_call_target="tpu_custom_call" | custom-call | flops 99999997952 | bytes 12000000 | tf_op jit(solution)/shard_map/invert/pallas_call | solution.py:478
  174.8 0.0 all-to-all-done
  174.8 5.5 %bitcast_convert_fusion = f32[384,32,128]{2,1,0:T(8,128)} fusion(bf16[128,3,32,128]{3,2,1,0:T(8,128)(2,1)} %all-to-all-done), kind=kLoop, calls=%fused_computation | loop fusion | flops 1572864 | bytes 9437184 | tf_op jit(solution)/shard_map/reshape | solution.py:528
  180.3 0.8 copy.11
  181.1 0.6 copy.12
Async XLA Ops:
  5.0 11.1 %copy-start = (bf16[96,3072]{1,0:T(8,128)(2,1)S(1)}, bf16[96,3072]{1,0:T(8,128)(2,1)}, u32[]{:S(2)}) copy-start(bf16[96,3072]{1,0:T(8,128)(2,1)} %panel_ref.1) | copy-start | bytes 1769476
  5.0 11.1 %copy-start.1 = (f32[96,96]{1,0:T(8,128)S(1)}, f32[96,96]{1,0:T(8,128)}, u32[]{:S(2)}) copy-start(f32[96,96]{1,0:T(8,128)} %dinv_ref.1) | copy-start | bytes 110596
  5.1 11.1 %copy-start.2 = (s32[2,192]{1,0:T(2,128)S(1)}, s32[2,192]{1,0:T(2,128)}, u32[]{:S(2)}) copy-start(s32[2,192]{1,0:T(2,128)} %mask_ref.1) | copy-start | bytes 4612
  5.1 169.7 %all-to-all-start = ((bf16[128,3,32,128]{3,2,1,0:T(8,128)(2,1)}), bf16[128,3,32,128]{3,2,1,0:T(8,128)(2,1)}, u32[]{:S(2)}, u32[]{:S(2)}) async-start(bf16[128,3,32,128]{3,2,1,0:T(8,128)(2,1)} %bitcast.5), calls=%async_computation | async-start | bytes 6291456 | tf_op jit(solution)/shard_map/all_to_all | solution.py:526

commit v4 on v3

--- a/solution.py
+++ b/solution.py
@@ -81,6 +81,49 @@
     )(owners, pieces)
 
 
+def widen_kernel(narrow_hbm, wide_hbm, narrow, wide, in_sems, out_sems):
+    parts, per = narrow.shape[:2]
+    arriving = [
+        pltpu.make_async_copy(narrow_hbm.at[pl.ds(i * per, per)], narrow.at[i], in_sems.at[i])
+        for i in range(parts)
+    ]
+    leaving = [
+        pltpu.make_async_copy(wide.at[i], wide_hbm.at[pl.ds(i * per, per)], out_sems.at[i])
+        for i in range(parts)
+    ]
+    for copy in arriving:
+        copy.start()
+    for i in range(parts):
+        arriving[i].wait()
+
+        def cast(j, _, i=i):
+            wide[i, pl.ds(j * 4, 4)] = narrow[i, pl.ds(j * 4, 4)].astype(F32)
+            return 0
+
+        lax.fori_loop(0, per // 4, cast, 0)
+        leaving[i].start()
+    for copy in leaving:
+        copy.wait()
+
+
+def widened(narrow):
+    parts = 8
+    inside = (parts, narrow.shape[0] // parts, *narrow.shape[1:])
+    return pl.pallas_call(
+        widen_kernel,
+        out_shape=jax.ShapeDtypeStruct(narrow.shape, F32),
+        in_specs=[pl.BlockSpec(memory_space=pl.ANY)],
+        out_specs=pl.BlockSpec(memory_space=pl.ANY),
+        scratch_shapes=[
+            pltpu.VMEM(inside, narrow.dtype),
+            pltpu.VMEM(inside, F32),
+            pltpu.SemaphoreType.DMA((parts,)),
+            pltpu.SemaphoreType.DMA((parts,)),
+        ],
+        name="widen",
+    )(narrow)
+
+
 def invert_kernel(
     mask_ref, a_hbm, panel_ref, dinv_ref, upper_ref, diag_ref,
     lmx, lm, a, part, in1, tot, in2, usend, ubuf, sendd, recvd,
@@ -268,6 +311,12 @@
 
     FAR, NEXT, LAST, OWN = range(4)
 
+    def hop1(half, slot, piece, n, step):
+        go(
+            part.at[half, slot, piece], in1.at[half, n], p1_ssem.at[half, n], p1_rsem.at[half, n],
+            *neighbour(half, step),
+        )
+
     def multiply(half, slot, dest, blocks_due=()):
         across, along = (SIDE, 1) if half == 0 else (1, SIDE)
 
@@ -291,12 +340,7 @@
                 return 0
 
             lax.fori_loop(0, SUBS, tile_and_part, 0)
-
-    def hop1(half, slot, piece, n, step):
-        go(
-            part.at[half, slot, piece], in1.at[half, n], p1_ssem.at[half, n], p1_rsem.at[half, n],
-            *neighbour(half, step),
-        )
+            hop1(half, slot, i, i, 1 + 2 * i)
 
     def add1(half, slot, piece, n):
         arrived(in1.at[half, n], p1_rsem.at[half, n])
@@ -311,8 +355,6 @@
 
     for half in range(2):
         multiply(half, FAR, (place[half] + 2) % SIDE, (4 + 2 * half, 5 + 2 * half))
-        hop1(half, FAR, 0, 0, 1)
-        hop1(half, FAR, 1, 1, 3)
     for n in range(4, 8):
         every_part(n, take)
     for half in range(2):
@@ -525,7 +567,7 @@
     parts = slots.reshape(devices, SLOT, *pieces.shape[1:])
     arrived = lax.all_to_all(parts, ("row", "col"), split_axis=0, concat_axis=0, tiled=True)
     upper, diag = inverted(struct_mask, ainv_anc, l_panel, diag_inv)
-    moved = arrived.astype(F32).reshape(slots.shape)
+    moved = widened(arrived.reshape(slots.shape))
     return upper, diag, moved
 
 

time: 182 us -> 181 us (level)
  other arithmetic: 5.49 us -> 0 us
  Pallas kernels: 163 us -> 167 us
    reshape x1 -> x0, other arithmetic: 5.49 us -> none  [local(): moved = arrived.astype(F32).reshape(slots.shape)]
    pallas_call x0 -> x1, Pallas kernels: none -> 3.89 us  [widened(): pl.pallas_call(widen_kernel, out_shape=jax.ShapeDtypeStruct(narrow.shape,...]
  transfers between devices with their start and end apart: 1 -> 1, of which waited for: 0 -> 0; matrix products, arithmetic and copies ran while one was open for 0% -> 0% of each run, Pallas kernels for 87% -> 88%
where the time goes in v4:
time: 181 us; the launch traced here: 180 us
  Pallas kernels  167 us (92%)
  starting transfers between devices  11.1 us (6%)
    pallas_call x1, Pallas kernels, inverted(): pl.pallas_call(invert_kernel, out_shape=(jax.ShapeDtypeStruct((rows, widt...  159 us
    all_to_all x1, starting transfers between devices, local(): lax.all_to_all(parts, ('row', 'col'), split_axis=0, concat_axis=0, tiled=...  11.1 us
    pallas_call x1, Pallas kernels, packed(): pl.pallas_call(pack_kernel, out_shape=jax.ShapeDtypeStruct((devices * SLO...  4.4 us
    pallas_call x1, Pallas kernels, widened(): pl.pallas_call(widen_kernel, out_shape=jax.ShapeDtypeStruct(narrow.shape,...  3.89 us
  transfers between devices with their start and end apart: 1, of which 0 were waited for; matrix products, arithmetic and copies ran while one was open for 0% of the time, Pallas kernels for 88%

profile of v4, /device:TPU:13, one launch (start us, length us, event | category | flops | bytes accessed | tf_op | source)
XLA Modules:
  0.0 180.4 jit_solution(7470359105202205536)
XLA Ops:
  0.6 4.4 %pack.1 = bf16[384,32,128]{2,1,0:T(8,128)(2,1)} custom-call(s32[192]{0:T(256)} %bitcast.4, f32[192,32,128]{2,1,0:T(8,128)} %pieces_hbm.1), custom_call_target="tpu_custom_call" | custom-call | tf_op jit(solution)/shard_map/pack/pallas_call | solution.py:66
  5.0 0.0 copy-start
  5.0 0.0 copy-start.1
  5.1 0.0 copy-start.2
  5.1 11.1 %all-to-all-start = ((bf16[128,3,32,128]{3,2,1,0:T(8,128)(2,1)}), bf16[128,3,32,128]{3,2,1,0:T(8,128)(2,1)}, u32[]{:S(2)}, u32[]{:S(2)}) async-start(bf16[128,3,32,128]{3,2,1,0:T(8,128)(2,1)} %bitcast.3), calls=%async_computation | async-start | bytes 6291456 | tf_op jit(solution)/shard_map/all_to_all | solution.py:568
  16.2 0.0 copy-done
  16.2 0.0 copy-done.1
  16.2 0.0 copy-done.2
  16.2 158.9 %invert.1 = (bf16[96,3072]{1,0:T(8,128)(2,1)S(1)}, f32[96,96]{1,0:T(8,128)S(1)}) custom-call(s32[2,192]{1,0:T(2,128)S(1)} %copy-done.2, bf16[3072,1536]{1,0:T(8,128)(2,1)} %a_hbm.1, bf16[96,3072]{1,0:T(8,128)(2,1)S(1)} %copy-done, f32[96,96]{1,0:T(8,128)S(1)} %copy-done.1), custom_call_target="tpu_custom_call" | custom-call | flops 99999997952 | bytes 12000000 | tf_op jit(solution)/shard_map/invert/pallas_call | solution.py:520
  175.1 0.0 all-to-all-done
  175.1 3.9 %widen.1 = f32[384,32,128]{2,1,0:T(8,128)} custom-call(bf16[384,32,128]{2,1,0:T(8,128)(2,1)} %bitcast.2.narrow_hbm), custom_call_target="tpu_custom_call" | custom-call | tf_op jit(solution)/shard_map/widen/pallas_call | solution.py:112
  179.0 0.8 copy.11
  179.8 0.6 copy.12
Async XLA Ops:
  5.0 11.1 %copy-start = (bf16[96,3072]{1,0:T(8,128)(2,1)S(1)}, bf16[96,3072]{1,0:T(8,128)(2,1)}, u32[]{:S(2)}) copy-start(bf16[96,3072]{1,0:T(8,128)(2,1)} %panel_ref.1) | copy-start | bytes 1769476
  5.0 11.1 %copy-start.1 = (f32[96,96]{1,0:T(8,128)S(1)}, f32[96,96]{1,0:T(8,128)}, u32[]{:S(2)}) copy-start(f32[96,96]{1,0:T(8,128)} %dinv_ref.1) | copy-start | bytes 110596
  5.1 11.1 %copy-start.2 = (s32[2,192]{1,0:T(2,128)S(1)}, s32[2,192]{1,0:T(2,128)}, u32[]{:S(2)}) copy-start(s32[2,192]{1,0:T(2,128)} %mask_ref.1) | copy-start | bytes 4612
  5.1 170.0 %all-to-all-start = ((bf16[128,3,32,128]{3,2,1,0:T(8,128)(2,1)}), bf16[128,3,32,128]{3,2,1,0:T(8,128)(2,1)}, u32[]{:S(2)}, u32[]{:S(2)}) async-start(bf16[128,3,32,128]{3,2,1,0:T(8,128)(2,1)} %bitcast.3), calls=%async_computation | async-start | bytes 6291456 | tf_op jit(solution)/shard_map/all_to_all | solution.py:568

commit v5 on v4

--- a/solution.py
+++ b/solution.py
@@ -317,7 +317,7 @@
             *neighbour(half, step),
         )
 
-    def multiply(half, slot, dest, blocks_due=()):
+    def multiply(half, slot, dest, blocks_due=(), direct=None):
         across, along = (SIDE, 1) if half == 0 else (1, SIDE)
 
         def tile(t, _):
@@ -330,7 +330,13 @@
             part[half, slot, t // per, :, pl.ds(pl.multiple_of((t % per) * TILE, TILE), TILE)] = value.astype(BF16)
             return 0
 
-        if not blocks_due:
+        per = QUART // TILE
+        if direct is not None:
+            piece, n, step = direct
+            lax.fori_loop(piece * per, (piece + 1) * per, tile, 0)
+            hop1(half, slot, piece, n, step)
+            lax.fori_loop((1 - piece) * per, (2 - piece) * per, tile, 0)
+        elif not blocks_due:
             lax.fori_loop(0, HALF // TILE, tile, 0)
         for i, n in enumerate(blocks_due):
 
@@ -358,10 +364,8 @@
     for n in range(4, 8):
         every_part(n, take)
     for half in range(2):
-        multiply(half, NEXT, (place[half] + 1) % SIDE)
-        hop1(half, NEXT, 1, 3, 1)
-        multiply(half, LAST, (place[half] + 3) % SIDE)
-        hop1(half, LAST, 0, 5, 3)
+        multiply(half, NEXT, (place[half] + 1) % SIDE, direct=(1, 3, 1))
+        multiply(half, LAST, (place[half] + 3) % SIDE, direct=(0, 5, 3))
     for half in range(2):
         add1(half, NEXT, 0, 0)
         hop1(half, NEXT, 0, 2, 1)

time: 181 us -> 179 us (0.989)
  no operation moved by 1% of the time
where the time goes in v5:
time: 179 us
  Pallas kernels  166 us (93%)
  starting transfers between devices  11.1 us (6%)
    pallas_call x1, Pallas kernels, inverted(): pl.pallas_call(invert_kernel, out_shape=(jax.ShapeDtypeStruct((rows, widt...  157 us
    all_to_all x1, starting transfers between devices, local(): lax.all_to_all(parts, ('row', 'col'), split_axis=0, concat_axis=0, tiled=...  11.1 us
    pallas_call x1, Pallas kernels, packed(): pl.pallas_call(pack_kernel, out_shape=jax.ShapeDtypeStruct((devices * SLO...  4.4 us
    pallas_call x1, Pallas kernels, widened(): pl.pallas_call(widen_kernel, out_shape=jax.ShapeDtypeStruct(narrow.shape,...  3.89 us
  transfers between devices with their start and end apart: 1, of which 0 were waited for; matrix products, arithmetic and copies ran while one was open for 0% of the time, Pallas kernels for 88%

profile of v5, /device:TPU:13, one launch (start us, length us, event | category | flops | bytes accessed | tf_op | source)
XLA Modules:
  0.0 179.0 jit_solution(3225146153906291109)
XLA Ops:
  0.6 4.4 %pack.1 = bf16[384,32,128]{2,1,0:T(8,128)(2,1)} custom-call(s32[192]{0:T(256)} %bitcast.4, f32[192,32,128]{2,1,0:T(8,128)} %pieces_hbm.1), custom_call_target="tpu_custom_call" | custom-call | tf_op jit(solution)/shard_map/pack/pallas_call | solution.py:66
  5.0 0.0 copy-start
  5.0 0.0 copy-start.1
  5.1 0.0 copy-start.2
  5.1 11.1 %all-to-all-start = ((bf16[128,3,32,128]{3,2,1,0:T(8,128)(2,1)}), bf16[128,3,32,128]{3,2,1,0:T(8,128)(2,1)}, u32[]{:S(2)}, u32[]{:S(2)}) async-start(bf16[128,3,32,128]{3,2,1,0:T(8,128)(2,1)} %bitcast.3), calls=%async_computation | async-start | bytes 6291456 | tf_op jit(solution)/shard_map/all_to_all | solution.py:572
  16.2 0.0 copy-done
  16.2 0.0 copy-done.1
  16.2 0.0 copy-done.2
  16.2 157.5 %invert.1 = (bf16[96,3072]{1,0:T(8,128)(2,1)S(1)}, f32[96,96]{1,0:T(8,128)S(1)}) custom-call(s32[2,192]{1,0:T(2,128)S(1)} %copy-done.2, bf16[3072,1536]{1,0:T(8,128)(2,1)} %a_hbm.1, bf16[96,3072]{1,0:T(8,128)(2,1)S(1)} %copy-done, f32[96,96]{1,0:T(8,128)S(1)} %copy-done.1), custom_call_target="tpu_custom_call" | custom-call | flops 99999997952 | bytes 12000000 | tf_op jit(solution)/shard_map/invert/pallas_call | solution.py:524
  173.7 0.0 all-to-all-done
  173.7 3.9 %widen.1 = f32[384,32,128]{2,1,0:T(8,128)} custom-call(bf16[384,32,128]{2,1,0:T(8,128)(2,1)} %bitcast.2.narrow_hbm), custom_call_target="tpu_custom_call" | custom-call | tf_op jit(solution)/shard_map/widen/pallas_call | solution.py:112
  177.6 0.8 copy.11
  178.4 0.6 copy.12
Async XLA Ops:
  5.0 11.1 %copy-start = (bf16[96,3072]{1,0:T(8,128)(2,1)S(1)}, bf16[96,3072]{1,0:T(8,128)(2,1)}, u32[]{:S(2)}) copy-start(bf16[96,3072]{1,0:T(8,128)(2,1)} %panel_ref.1) | copy-start | bytes 1769476
  5.0 11.1 %copy-start.1 = (f32[96,96]{1,0:T(8,128)S(1)}, f32[96,96]{1,0:T(8,128)}, u32[]{:S(2)}) copy-start(f32[96,96]{1,0:T(8,128)} %dinv_ref.1) | copy-start | bytes 110596
  5.1 11.1 %copy-start.2 = (s32[2,192]{1,0:T(2,128)S(1)}, s32[2,192]{1,0:T(2,128)}, u32[]{:S(2)}) copy-start(s32[2,192]{1,0:T(2,128)} %mask_ref.1) | copy-start | bytes 4612
  5.1 168.6 %all-to-all-start = ((bf16[128,3,32,128]{3,2,1,0:T(8,128)(2,1)}), bf16[128,3,32,128]{3,2,1,0:T(8,128)(2,1)}, u32[]{:S(2)}, u32[]{:S(2)}) async-start(bf16[128,3,32,128]{3,2,1,0:T(8,128)(2,1)} %bitcast.3), calls=%async_computation | async-start | bytes 6291456 | tf_op jit(solution)/shard_map/all_to_all | solution.py:572
